TPU v7x, 512 devices: a whole 4x8x8 slice. The times are simulated.
512 devices in a mesh: hot: 16 (over z, core), cold: 32 (over x, y).
Axes of the slice: x: 4, y: 8, z: 8, core: 2. Of those that a mesh axis runs over, the one named last changes fastest.
Arguments:
- tokens: bfloat16 [512, 8192], P('cold', 'hot'), may hold values from -6 to 6
- hot_gate: bfloat16 [8192, 4096], P('hot', 'cold'), may hold values from -0.0625 to 0.0625
- hot_up: bfloat16 [8192, 4096], P('hot', 'cold'), may hold values from -0.0625 to 0.0625
- hot_down: bfloat16 [4096, 8192], P('cold', 'hot'), may hold values from -0.0625 to 0.0625
- cold_gate: bfloat16 [8192, 24576], P('hot', 'cold'), may hold values from -0.0625 to 0.0625
- cold_up: bfloat16 [8192, 24576], P('hot', 'cold'), may hold values from -0.0625 to 0.0625
- cold_down: bfloat16 [24576, 8192], P('cold', 'hot'), may hold values from -0.0625 to 0.0625
- hot_ids: int32 [32], replicated, may hold values from 0 to 223, as said below
- cold_ids: int32 [192], replicated, may hold values from 0 to 223, as said below
- block_mask: int32 [512, 224], replicated, may hold values from 0 to 1, as said below
Outputs:
- mixed: bfloat16 [512, 8192], P('cold', 'hot')
Inputs may be any that keep to these rules, and one draw needn't show every extreme that they name: hot_ids and cold_ids together name every block number from 0 to 223 once. `cold_ids`: cold slot s lies with index s // 6 of cold. `block_mask`: among the 16 tokens of one index of cold, at most 8 have a 1 in a cold slot of one given index of cold; in every draw some index of cold gets exactly 8 such tokens from every index of cold.
All inputs are finite; a program needn't handle non-finite values.
Results may differ from a plain program's by a relative error of at most 0.0049.
Values may be sent and summed in bfloat16 or wider, within the bound.
A program may use at most 64 MiB of HBM per device.

v0:
```python
import jax
import jax.numpy as jnp
from jax import lax
from jax.sharding import PartitionSpec as P

BLOCK = 128


def sent_to_all(array, axis):
    copies = jnp.broadcast_to(array, (lax.axis_size(axis), *array.shape))
    return lax.all_to_all(copies, axis, split_axis=0, concat_axis=0, tiled=True)


def laid_out(tiles, dim):
    tiles = jnp.moveaxis(tiles, 0, dim)
    dims = tiles.shape
    return tiles.reshape(*dims[:dim], dims[dim] * dims[dim + 1], *dims[dim + 2 :])


def gather_directly(array, axis, dim):
    tiles = sent_to_all(array, axis)
    return laid_out(tiles, dim)


def split_up(array, dim, size):
    dims = array.shape
    tiles = array.reshape(*dims[:dim], size, dims[dim] // size, *dims[dim + 1 :])
    return jnp.moveaxis(tiles, dim, 0)


def sum_packed(arrays, axis, dims):
    size = lax.axis_size(axis)
    tiles = [split_up(a, dim, size) for a, dim in zip(arrays, dims)]
    lines = jnp.concatenate([b.reshape(size, -1) for b in tiles], axis=1)
    extent = max(16, -(-lines.shape[1] // 1024) * 8)
    lines = jnp.pad(lines, ((0, 0), (0, extent * 128 - lines.shape[1]))).reshape(-1, 128)
    line, at, finished = (lax.psum_scatter(lines, axis, tiled=True).reshape(-1), 0, [])
    for b in tiles:
        part = b[0]
        finished.append(line[at : at + part.size].reshape(part.shape))
        at += part.size
    return tuple(finished)


def gather_packed(arrays, axis, dims):
    line = jnp.concatenate([a.reshape(-1) for a in arrays])
    lines, at, finished = (lax.all_gather(line, axis), 0, [])
    for a, dim in zip(arrays, dims):
        tiles = lines[:, at : at + a.size].reshape(-1, *a.shape)
        finished.append(laid_out(tiles, dim))
        at += a.size
    return tuple(finished)


def sum_at_owner(array, axis, dim):
    tiles = split_up(array, dim, lax.axis_size(axis))
    arrived = lax.all_to_all(tiles, axis, split_axis=0, concat_axis=0, tiled=True)
    return arrived.sum(axis=0)


def expand_bits(block_bits):
    row_total = block_bits.shape[0]
    widened = jnp.broadcast_to(
        block_bits.astype(jnp.float32)[:, :, None], (row_total, block_bits.shape[1], BLOCK)
    )
    return widened.reshape(row_total, block_bits.shape[1] * BLOCK)


def gated_hidden(gate_sum, up_sum, block_bits):
    return (jax.nn.silu(gate_sum) * up_sum * expand_bits(block_bits)).astype(jnp.bfloat16)


def body(
    tokens, hot_gate, hot_up, hot_down, cold_gate, cold_up, cold_down, hot_ids, cold_ids, block_mask
):
    groups = lax.axis_size("cold")
    own_group = lax.axis_index("cold")
    local_rows = tokens.shape[0]
    slot_count = local_rows // 2
    all_rows = block_mask.shape[0]
    feature_cols = tokens.shape[1]
    hot_width = hot_gate.shape[1]
    hot_blocks = hot_width // BLOCK
    cold_blocks = cold_gate.shape[1] // BLOCK
    slot_rows = groups * slot_count
    cold_bits = jnp.take(block_mask, cold_ids, axis=1)
    group_hits = jnp.max(cold_bits.reshape(all_rows, groups, cold_blocks), axis=2)
    source_hits = group_hits.reshape(groups, local_rows, groups)
    slot_index = jnp.cumsum(source_hits, axis=1) - source_hits
    my_hits = lax.dynamic_index_in_dim(source_hits, own_group, 0, keepdims=False)
    my_slots = lax.dynamic_index_in_dim(slot_index, own_group, 0, keepdims=False)
    slot_range = jnp.arange(slot_count, dtype=jnp.int32)
    chosen = (my_slots.T[:, None, :] == slot_range[None, :, None]) & (my_hits.T[:, None, :] > 0)
    chosen = chosen.astype(jnp.bfloat16)
    outgoing = jnp.einsum("gst,td->gsd", chosen, tokens, preferred_element_type=jnp.float32).astype(
        jnp.bfloat16
    )
    arrived = lax.all_to_all(outgoing, "cold", split_axis=0, concat_axis=0, tiled=True)
    arrived = arrived.reshape(slot_rows, feature_cols)
    own_hits = lax.dynamic_index_in_dim(source_hits, own_group, 2, keepdims=False)
    own_slots = lax.dynamic_index_in_dim(slot_index, own_group, 2, keepdims=False)
    source_base = jnp.arange(groups, dtype=jnp.int32)[:, None] * slot_count
    target = jnp.where(own_hits > 0, source_base + own_slots, slot_rows).reshape(all_rows)
    row_token = (
        jnp.full((slot_rows + 1,), all_rows, jnp.int32)
        .at[target]
        .set(jnp.arange(all_rows, dtype=jnp.int32))[:slot_rows]
    )
    own_bits = lax.dynamic_slice_in_dim(cold_bits, own_group * cold_blocks, cold_blocks, 1)
    padded_bits = jnp.concatenate([own_bits, jnp.zeros((1, cold_blocks), own_bits.dtype)], axis=0)
    arrived_bits = jnp.take(padded_bits, row_token, axis=0)
    my_hot = lax.dynamic_slice_in_dim(hot_ids, own_group * hot_blocks, hot_blocks, 0)
    hot_bits = jnp.take(block_mask, my_hot, axis=1)
    both_hot = jnp.concatenate([hot_gate, hot_up], axis=1)
    hot_parts = jnp.dot(
        gather_directly(tokens, "cold", 0), both_hot, preferred_element_type=jnp.float32
    )
    hot_gates = hot_parts[:, :hot_width]
    hot_ups = hot_parts[:, hot_width:]
    cold_gates = jnp.dot(arrived, cold_gate, preferred_element_type=jnp.float32)
    cold_ups = jnp.dot(arrived, cold_up, preferred_element_type=jnp.float32)
    shares = lax.axis_size("hot")
    part_index = lax.axis_index("hot")
    hot_gates, hot_ups, cold_gates, cold_ups = sum_packed(
        (hot_gates, hot_ups, cold_gates, cold_ups), "hot", (0, 0, 0, 0)
    )
    hot_share = all_rows // shares
    cold_share = slot_rows // shares
    hot_part_bits = lax.dynamic_slice_in_dim(hot_bits, part_index * hot_share, hot_share, 0)
    cold_part_bits = lax.dynamic_slice_in_dim(arrived_bits, part_index * cold_share, cold_share, 0)
    hot_piece = gated_hidden(hot_gates, hot_ups, hot_part_bits)
    cold_piece = gated_hidden(cold_gates, cold_ups, cold_part_bits)
    hot_hidden, cold_hidden = gather_packed((hot_piece, cold_piece), "hot", (0, 0))
    cold_out = jnp.dot(cold_hidden, cold_down, preferred_element_type=jnp.float32)
    placed = (
        jnp.zeros((all_rows + 1, feature_cols), jnp.float32).at[row_token].add(cold_out)[:all_rows]
    )
    partial_value = jnp.dot(hot_hidden, hot_down, preferred_element_type=jnp.float32)
    partial_value = partial_value + placed
    combined = sum_at_owner(partial_value, "cold", 0)
    return combined.astype(jnp.bfloat16)


def solution(mesh):
    return jax.shard_map(
        body,
        mesh=mesh,
        in_specs=(
            P("cold", "hot"),
            P("hot", "cold"),
            P("hot", "cold"),
            P("cold", "hot"),
            P("hot", "cold"),
            P("hot", "cold"),
            P("cold", "hot"),
            P(),
            P(),
            P(),
        ),
        out_specs=P("cold", "hot"),
        check_vma=False,
    )
```

profile of v0, /device:TPU:1, one launch (start us, length us, event | category | flops | bytes accessed | tf_op | source)
XLA Modules:
  0.0 189.6 jit_solution(11409266597436794511)
XLA Ops:
  6.5 0.0 copy-start
  6.5 0.8 compare_and_fusion.1
  7.3 0.7 compare_select_fusion.2
  8.0 0.1 broadcast_in_dim.74
  8.1 2.1 %gather_fusion = s32[192,512]{1,0:T(8,128)S(1)} fusion(s32[512,224]{0,1:T(8,128)} %param.19, s32[1024]{0:T(1024)S(1)} %pad_clamp_fusion.1), kind=kCustom, calls=%fused_computation | custom fusion | bytes 787200 | tf_op jit(solution)/shard_map/jit(_take)/gather | solution.py:86
  10.2 0.0 copy-start.7
  10.2 0.1 gather.15
  10.2 0.3 select_reduce_fusion
  10.5 0.1 copy.23
  10.7 0.1 reduce-window_subtract_fusion
  10.8 0.1 copy.27
  10.9 0.1 copy.26
  11.0 0.0 copy-done.7
  11.0 0.2 convolution_convert_fusion
  11.2 20.0 %all_to_all.15 = bf16[32,8,512]{2,1,0:T(8,128)(2,1)S(1)} all-to-all(bf16[32,8,512]{2,1,0:T(8,128)(2,1)S(1)} %convolution_convert_fusion), channel_id=1, replica_groups=mesh['hot'=16,'cold'=32] {'cold'}, dimensions={0} | all-to-all | bytes 524288 | tf_op jit(solution)/shard_map/all_to_all | solution.py:98
  31.2 0.9 broadcast_in_dim.73
  32.0 6.3 %all-to-all-start = ((bf16[32,16,512]{2,1,0:T(8,128)(2,1)}), bf16[32,16,512]{2,1,0:T(8,128)(2,1)S(1)}, u32[]{:S(2)}, u32[]{:S(2)}) async-start(bf16[32,16,512]{2,1,0:T(8,128)(2,1)} %broadcast_in_dim.73), calls=%async_computation | async-start | bytes 1048576 | tf_op jit(solution)/shard_map/all_to_all | solution.py:11
  38.4 0.0 copy-done.1
  38.4 0.0 reduce-scatter.2.cloned.1.call-start
  38.5 0.4 fusion.5
  38.8 1.0 reshape_reshape.21
  39.9 1.5 fusion.7
  41.4 1.0 reshape_reshape.20
  42.5 9.0 %all-to-all-done = bf16[32,16,512]{2,1,0:T(8,128)(2,1)S(1)} async-done(((bf16[32,16,512]{2,1,0:T(8,128)(2,1)}), bf16[32,16,512]{2,1,0:T(8,128)(2,1)S(1)}, u32[]{:S(2)}, u32[]{:S(2)}) %all-to-all-start) | async-done | bytes 524320 | tf_op jit(solution)/shard_map/all_to_all | solution.py:11
  51.5 0.3 convolution_bitcast_fusion
  51.9 0.1 copy.21
  52.0 0.8 reshape_reshape.18
  52.8 0.1 copy.22
  52.9 0.8 reshape_reshape.19
  53.6 1.6 pad_maximum_fusion
  55.3 1.5 reshape.135
  56.8 0.0 reduce-scatter.2.cloned.1.call-update
  56.8 0.6 copy-done.8
  57.5 0.6 dynamic_slice.28
  60.0 0.1 dynamic-slice.7
  60.1 0.1 add.96
  60.2 0.1 add.97
  60.2 0.7 fusion.10
  61.0 0.1 gt.38
  61.1 0.1 constant_dynamic-slice_fusion
  61.2 0.3 copy.28
  61.5 0.1 squeeze.11
  61.6 0.1 dynamic-slice_select_fusion
  61.7 0.2 copy.30
  61.9 2.4 %scatter_custom_fusion = s32[257]{0:T(512)S(1)} fusion(s32[512]{0:T(512)S(1)} %bitcast.60, s32[512]{0:T(512)S(1)} %iota.13, s32[]{:T(128)} %constant.70.clone.1), kind=kCustom, calls=%fused_computation.51 | custom fusion | bytes 1032 | tf_op jit(solution)/shard_map/scatter | solution.py:107
  64.3 0.1 dynamic-slice.8
  64.4 0.7 gather_fusion.1
  65.2 0.1 fusion.21
  65.2 0.1 broadcast_in_dim.89
  65.3 0.8 fusion.27
  66.2 56.0 %reduce-scatter.2.cloned.1.call-done = f32[256,128]{1,0:T(8,128)} async-done(((f32[4096,128]{1,0:T(8,128)}), f32[256,128]{1,0:T(8,128)}) %reduce-scatter.2.cloned.1.call-update) | async-done | bytes 131088 | tf_op jit(solution)/shard_map/reduce_scatter | solution.py:37
  122.2 0.8 fusion.17
  123.0 0.8 fusion.23
  123.8 19.0 %all-gather = bf16[262144]{0:T(1024)(128)(2,1)S(1)} all-gather(bf16[16384]{0:T(1024)(128)(2,1)S(1)} %pad_maximum_fusion.1), channel_id=2, replica_groups=mesh['hot'=16,'cold'=32] {'hot'}, dimensions={0}, use_global_device_ids=true | all-gather | bytes 557056 | tf_op jit(solution)/shard_map/all_gather | solution.py:47
  142.9 0.2 reshape.214
  143.1 0.0 copy-start.6
  143.2 0.2 reshape_reshape.23
  143.3 0.1 reshape_reshape.22
  143.4 0.0 copy-done.3
  143.4 1.2 fusion.30
  144.6 2.9 %scatter_custom_fusion.1 = f32[513,512]{1,0:T(8,128)S(1)} fusion(s32[256]{0:T(256)S(1)} %compare_select_fusion.1, f32[256,512]{1,0:T(8,128)} %fusion.30, f32[]{:T(128)} %constant.101.clone.1), kind=kCustom, calls=%fused_computation.9 | custom fusion | flops 131072 | bytes 1051136 | tf_op jit(solution)/shard_map/scatter-add | solution.py:136
  147.5 0.3 convolution_add_fusion
  147.8 34.3 %all_to_all.16 = f32[32,16,512]{2,1,0:T(8,128)S(1)} all-to-all(f32[32,16,512]{2,1,0:T(8,128)S(1)} %bitcast.52), channel_id=1, replica_groups=mesh['hot'=16,'cold'=32] {'cold'}, dimensions={0} | all-to-all | bytes 2097152 | tf_op jit(solution)/shard_map/all_to_all | solution.py:57
  182.1 0.7 reduce_sum.9
  (26 shorter events, 0.2 us)
Async XLA Ops:
  6.5 31.9 %copy-start = (bf16[512,768]{1,0:T(8,128)(2,1)S(1)}, bf16[512,768]{1,0:T(8,128)(2,1)}, u32[]{:S(2)}) copy-start(bf16[512,768]{1,0:T(8,128)(2,1)} %param.15) | copy-start | bytes 2359300
  10.2 0.8 copy-start.7
  10.8 27.6 %copy-start.1 = (s32[32,16,32]{2,0,1:T(8,128)}, s32[32,16,32]{2,0,1:T(8,128)S(1)}, u32[]{:S(2)}) copy-start(s32[32,16,32]{2,0,1:T(8,128)S(1)} %reduce-window_subtract_fusion) | copy-start | bytes 196612
  32.0 19.4 %all-to-all-start = ((bf16[32,16,512]{2,1,0:T(8,128)(2,1)}), bf16[32,16,512]{2,1,0:T(8,128)(2,1)S(1)}, u32[]{:S(2)}, u32[]{:S(2)}) async-start(bf16[32,16,512]{2,1,0:T(8,128)(2,1)} %broadcast_in_dim.73), calls=%async_computation | async-start | bytes 1048576 | tf_op jit(solution)/shard_map/all_to_all | solution.py:11
  38.4 83.8 %reduce-scatter.2.cloned.1.call-start = ((), (), s32[]{:S(2)}) async-start(), calls=%async_computation.4 | async-start | bytes 2228224 | tf_op jit(solution)/shard_map/reduce_scatter | solution.py:37
  39.9 11.6 %copy-start.4 = (bf16[512,128]{1,0:T(8,128)(2,1)S(1)}, bf16[512,128]{1,0:T(8,128)(2,1)}, u32[]{:S(2)}) copy-start(bf16[512,128]{1,0:T(8,128)(2,1)} %param.12) | copy-start | bytes 393220
  39.9 11.6 %copy-start.5 = (bf16[512,128]{1,0:T(8,128)(2,1)S(1)}, bf16[512,128]{1,0:T(8,128)(2,1)}, u32[]{:S(2)}) copy-start(bf16[512,128]{1,0:T(8,128)(2,1)} %param.11) | copy-start | bytes 393220
  56.8 0.7 copy-start.8
  56.8 4.3 %copy-start.2 = (s32[32,16,32]{2,0,1:T(8,128)S(1)}, s32[32,16,32]{2,0,1:T(8,128)}, u32[]{:S(2)}) copy-start(s32[32,16,32]{2,0,1:T(8,128)} %copy-done.1) | copy-start | bytes 196612
  65.2 78.3 %copy-start.3 = (bf16[768,512]{1,0:T(8,128)(2,1)S(1)}, bf16[768,512]{1,0:T(8,128)(2,1)}, u32[]{:S(2)}) copy-start(bf16[768,512]{1,0:T(8,128)(2,1)} %param.16) | copy-start | bytes 2359300
  143.1 4.3 %copy-start.6 = (bf16[128,512]{1,0:T(8,128)(2,1)S(1)}, bf16[128,512]{1,0:T(8,128)(2,1)}, u32[]{:S(2)}) copy-start(bf16[128,512]{1,0:T(8,128)(2,1)} %param.13) | copy-start | bytes 393220
Sparse Core Ops, SparseCore 0:
  57.0 65.1 reduce-scatter.1
where the time goes:
time: 193 us; the launch traced here: 190 us
  blocking collectives  73.3 us (38%)
  waiting for transfers between devices  65 us (34%)
  between operations  15.7 us (8%)
  local copies, waits for them, and re-layouts  14.9 us (8%)
  other arithmetic  10.4 us (5%)
  starting transfers between devices  6.39 us (3%)
  matrix products  3.89 us (2%)
    reduce_scatter x1, waiting for transfers between devices, sum_packed(): lax.psum_scatter(lines, axis, tiled=True).reshape(-1)  56 us
    all_to_all x1, blocking collectives, sum_at_owner(): lax.all_to_all(tiles, axis, split_axis=0, concat_axis=0, tiled=True)  34.3 us
    all_to_all x1, blocking collectives, body(): lax.all_to_all(outgoing, 'cold', split_axis=0, concat_axis=0, tiled=True)  20 us
    all_gather x1, blocking collectives, gather_packed(): lines, at, finished = (lax.all_gather(line, axis), 0, [])  19 us
    all_to_all x1, waiting for transfers between devices, sent_to_all(): return lax.all_to_all(copies, axis, split_axis=0, concat_axis=0, tiled=True)  9 us
    all_to_all x1, starting transfers between devices, sent_to_all(): return lax.all_to_all(copies, axis, split_axis=0, concat_axis=0, tiled=True)  6.35 us
  transfers between devices with their start and end apart: 2, of which 2 were waited for; matrix products, arithmetic and copies ran while one was open for 6% of the time, Pallas kernels for 0%

commit v1 on v0

v1 whole, which is shorter than its diff:
```python
import jax
import jax.numpy as jnp
from jax import lax
from jax.experimental import pallas as pl
from jax.experimental.pallas import tpu as pltpu
from jax.sharding import PartitionSpec as P

BLOCK = 128
NX, NY, NZ = 4, 8, 8
STEPS = 4
CAP = 8
ROWS = 16
TOK = NX * ROWS
SLOTS = NX * CAP
COLD = 6
F32, BF16 = jnp.float32, jnp.bfloat16
ORDER = ((0, 2, 6, 4), (1, 7, 3, 5))
SEND_ORDER = (0, 1, 2, 7, 6, 3, 4, 5)
FAR_FIRST = (4, 3, 5, 2, 6, 1, 7)
MESH = pl.DeviceIdType.MESH


def dot(a, b):
    return jnp.dot(a, b, preferred_element_type=F32)


def kernel(
    tok, hot_gate, hot_up, hot_down, cold_gate, cold_up, cold_down, hot_ids, cold_ids, mask,
    out,
    tokv, xbuf, wcg, wcu, wh, wd, mord, ptab, pmat, mz, sbuf, sown, rbuf, hbuf, obuf, oown, dbuf, ebuf, fbuf,
    tok_sem, mask_sem, wl_sem, ws_sem, wr_sem,
    a1s, a1z, a1r, a2s, a2r, bs, br, cs, cr, d1s, d1r, d2s, d2z, d2r, d2zr,
):
    hot, cold = lax.axis_index("hot"), lax.axis_index("cold")
    z, k = lax.div(hot, 2), lax.rem(hot, 2)
    x, y = lax.div(cold, NY), lax.rem(cold, NY)
    feat = tok.shape[1]

    def dev(px, py, pz, pk):
        return {"hot": pz * 2 + pk, "cold": px * NY + py}

    def at_x(d):
        return lax.rem(x + (d % NX), NX)

    def at_y(d):
        return lax.rem(y + NY + d, NY)

    def at_z(d):
        return lax.rem(z + (d % NZ), NZ)

    def dy_of(s):
        return ORDER[0][s] + k * (ORDER[1][s] - ORDER[0][s])

    def remote(src, dst, send, recv, to):
        return pltpu.make_async_remote_copy(
            src_ref=src, dst_ref=dst, send_sem=send, recv_sem=recv, device_id=to, device_id_type=MESH
        )

    here = dev(x, y, z, k)
    sister = dev(x, y, z, 1 - k)
    cols = pl.ds(pl.multiple_of(k * feat, feat), feat)
    mine = pl.ds(pl.multiple_of(k * feat, feat), feat)

    barrier = pltpu.get_barrier_semaphore()

    def greet(to):
        pl.semaphore_signal(barrier, inc=1, device_id=to, device_id_type=MESH)

    for d in range(1, NY):
        greet(dev(x, at_y(d), z, 0))
        greet(dev(x, at_y(d), z, 1))
    for d in range(1, NX):
        greet(dev(at_x(d), y, z, k))
    for d in range(1, NZ):
        greet(dev(x, y, at_z(d), k))
    greet(sister)

    tok_load = pltpu.make_async_copy(tok, tokv, tok_sem)
    tok_load.start()
    for s in range(STEPS):
        for dx in range(NX):
            group = at_x(dx) * NY + at_y(dy_of(s))
            pltpu.make_async_copy(
                mask.at[pl.ds(pl.multiple_of(group * ROWS, ROWS), ROWS), :],
                mord.at[pl.ds(s * TOK + dx * ROWS, ROWS), :],
                mask_sem,
            ).start()
    pieces = (
        (cold_gate, wcg.at[mine, :]),
        (cold_up, wcu.at[mine, :]),
        (hot_gate, wh.at[mine, pl.ds(0, BLOCK)]),
        (hot_up, wh.at[mine, pl.ds(BLOCK, BLOCK)]),
        (cold_down, wd.at[pl.ds(0, COLD * BLOCK), cols]),
        (hot_down, wd.at[pl.ds(COLD * BLOCK, BLOCK), cols]),
    )
    local_w = [pltpu.make_async_copy(a, b, wl_sem.at[i]) for i, (a, b) in enumerate(pieces)]
    remote_w = [remote(a, b, ws_sem.at[i], wr_sem.at[i], sister) for i, (a, b) in enumerate(pieces)]
    for copy in local_w:
        copy.start()

    pltpu.make_async_copy(mord, mord, mask_sem).wait()
    bits = mord[...].astype(F32).astype(BF16)
    blocks = mord.shape[1]
    block_no = lax.broadcasted_iota(jnp.int32, (blocks, BLOCK), 0)
    cold_sel = jnp.zeros((blocks, BLOCK), F32)
    for j in range(COLD):
        cold_sel = cold_sel + jnp.where(block_no == cold_ids[cold * COLD + j], 1.0, 0.0)
    unit_id = jnp.where(z < COLD, cold_ids[cold * COLD + jnp.minimum(z, COLD - 1)], hot_ids[cold])
    unit_sel = jnp.where(block_no == unit_id, 1.0, 0.0)
    hit = jnp.minimum(dot(bits, cold_sel.astype(BF16)), 1.0)
    unit_bit = dot(bits, unit_sel.astype(BF16))
    total = STEPS * TOK
    row = lax.broadcasted_iota(jnp.int32, (total, total), 0)
    col = lax.broadcasted_iota(jnp.int32, (total, total), 1)
    earlier = (lax.div(row, ROWS) == lax.div(col, ROWS)) & (col < row)
    slot = dot(jnp.where(earlier, 1.0, 0.0).astype(BF16), hit.astype(BF16))
    row = lax.broadcasted_iota(jnp.int32, (total, BLOCK), 0)
    lane = lax.broadcasted_iota(jnp.int32, (total, BLOCK), 1)
    base = lax.rem(lax.div(row, ROWS), NX) * CAP
    chosen = jnp.where((slot + base.astype(F32) == lane.astype(F32)) & (hit > 0.5), 1.0, 0.0)
    for s in range(STEPS):
        step_rows = slice(s * TOK, (s + 1) * TOK)
        pick = chosen[step_rows]
        ptab[s] = pick.astype(BF16)
        turned = jnp.transpose(pick)[:SLOTS].astype(BF16)
        pmat[s] = turned
        tokens_bit = unit_bit[step_rows]
        slot_bit = dot(turned, tokens_bit.astype(BF16))
        half_bit = jnp.where(z == COLD, tokens_bit[:SLOTS], tokens_bit[SLOTS:])
        mz[s] = jnp.where(z < COLD, slot_bit, half_bit)

    tok_load.wait()
    pl.semaphore_wait(barrier, 2 * (NY - 1) + (NX - 1) + (NZ - 1) + 1)

    for dy in SEND_ORDER:
        core = dy % 2
        s = ORDER[core].index(dy)
        spot = xbuf.at[s, pl.ds(0, ROWS), cols]
        if dy:
            remote(tokv, spot, a1s, a1r.at[s], dev(x, at_y(-dy), z, core)).start()
        else:

            @pl.when(k == 0)
            def _():
                pltpu.make_async_copy(tok, xbuf.at[0, pl.ds(0, ROWS), pl.ds(0, feat)], a1r.at[0]).start()

            @pl.when(k == 1)
            def _():
                remote(
                    tokv, xbuf.at[0, pl.ds(0, ROWS), pl.ds(feat, feat)], a1z, a1r.at[0], sister
                ).start()

    for copy in remote_w:
        copy.start()

    for s in range(STEPS):
        head = xbuf.at[s, pl.ds(0, ROWS), :]
        remote(head, head, a2s.at[s], a1r.at[s], here).wait_recv()
        for dx in (2, 1, 3):
            remote(
                head, xbuf.at[s, pl.ds(dx * ROWS, ROWS), :], a2s.at[s], a2r.at[s], dev(at_x(-dx), y, z, k)
            ).start()

    for s in range(STEPS):
        rest = xbuf.at[s, pl.ds(ROWS, TOK - ROWS), :]
        remote(rest, rest, a2s.at[s], a2r.at[s], here).wait_recv()
        if s == 0:
            for i in range(4):
                local_w[i].wait()
                remote_w[i].wait_recv()
        rows = xbuf[s]
        picked = dot(pmat[s], rows).astype(BF16)
        gates, ups = dot(picked, wcg[...]), dot(picked, wcu[...])
        hots = dot(rows, wh[...])
        for j in range(NZ):
            if j < COLD:
                part = slice(j * BLOCK, (j + 1) * BLOCK)
                gate, up = gates[:, part], ups[:, part]
            else:
                part = slice((j - COLD) * SLOTS, (j - COLD + 1) * SLOTS)
                gate, up = hots[part, :BLOCK], hots[part, BLOCK:]
            sown[s, j, :, :BLOCK] = gate
            sown[s, j, :, BLOCK:] = up
            sbuf[s, j, :, :BLOCK] = gate.astype(BF16)
            sbuf[s, j, :, BLOCK:] = up.astype(BF16)
        for dz in FAR_FIRST:
            remote(
                sbuf.at[s, at_z(dz)], rbuf.at[s, dz - 1], bs.at[s], br.at[s], dev(x, y, at_z(dz), k)
            ).start()

    for s in range(STEPS):
        remote(rbuf.at[s], rbuf.at[s], bs.at[s], br.at[s], here).wait_recv()
        terms = sown[s, z]
        for i in range(NZ - 1):
            terms = terms + rbuf[s, i].astype(F32)
        gate, up = terms[:, :BLOCK], terms[:, BLOCK:]
        hidden = gate / (1.0 + jnp.exp(-gate)) * up * mz[s]
        hbuf[s, z] = hidden.astype(BF16)
        for dz in FAR_FIRST:
            remote(
                hbuf.at[s, z], hbuf.at[s, z], cs.at[s], cr.at[s], dev(x, y, at_z(dz), k)
            ).start()

    for s in range(STEPS):
        most = hbuf.at[s, pl.ds(0, NZ - 1)]
        remote(most, most, cs.at[s], cr.at[s], here).wait_recv()
        if s == 0:
            for i in (4, 5):
                local_w[i].wait()
                remote_w[i].wait_recv()
        colds = jnp.concatenate([hbuf[s, j] for j in range(COLD)], axis=1)
        spread = dot(ptab[s][:, :SLOTS], colds).astype(BF16)
        hots = jnp.concatenate([hbuf[s, COLD], hbuf[s, COLD + 1]], axis=0)
        result = dot(spread, wd[: COLD * BLOCK, :]) + dot(hots, wd[COLD * BLOCK :, :])
        oown[s] = result[:ROWS]
        obuf[s] = result.astype(BF16)
        for dx in (2, 1, 3):
            remote(
                obuf.at[s, pl.ds(dx * ROWS, ROWS), :], dbuf.at[s, dx - 1], d1s.at[s], d1r.at[s],
                dev(at_x(dx), y, z, k),
            ).start()

    for s in range(STEPS):
        remote(dbuf.at[s], dbuf.at[s], d1s.at[s], d1r.at[s], here).wait_recv()
        terms = oown[s]
        for i in range(NX - 1):
            terms = terms + dbuf[s, i].astype(F32)
        ebuf[s, 0] = terms[:, :feat].astype(BF16)
        ebuf[s, 1] = terms[:, feat:].astype(BF16)
        dy = dy_of(s)

        def to_owners():
            for f in range(2):
                remote(
                    ebuf.at[s, f], fbuf.at[dy], d2s.at[s], d2r, dev(x, at_y(dy), z, f)
                ).start()

        if s:
            to_owners()
        else:
            pl.when(k == 1)(to_owners)

            @pl.when(k == 0)
            def _():
                remote(ebuf.at[0, 1], fbuf.at[0], d2z, d2zr, sister).start()
                fbuf[0] = terms[:, :feat].astype(BF16)

    remote(fbuf.at[pl.ds(1, NY - 1)], fbuf.at[pl.ds(1, NY - 1)], a1s, d2r, here).wait_recv()

    @pl.when(k == 1)
    def _():
        remote(fbuf.at[0], fbuf.at[0], d2z, d2zr, here).wait_recv()

    answer = fbuf[0].astype(F32)
    for dy in range(1, NY):
        answer = answer + fbuf[dy].astype(F32)
    out[...] = answer.astype(BF16)

    seven = fbuf.at[pl.ds(1, NY - 1)]
    remote(seven, seven, a1s, d2r, here).wait_send()
    for copy in remote_w:
        copy.wait_send()
    for s in range(STEPS):
        rest = xbuf.at[s, pl.ds(ROWS, TOK - ROWS), :]
        remote(rest, rest, a2s.at[s], a2r.at[s], here).wait_send()
        remote(rbuf.at[s], rbuf.at[s], bs.at[s], br.at[s], here).wait_send()
        most = hbuf.at[s, pl.ds(0, NZ - 1)]
        remote(most, most, cs.at[s], cr.at[s], here).wait_send()
        remote(dbuf.at[s], dbuf.at[s], d1s.at[s], d1r.at[s], here).wait_send()
        if s:
            remote(ebuf.at[s], ebuf.at[s], d2s.at[s], d2r, here).wait_send()

    @pl.when(k == 1)
    def _():
        remote(ebuf.at[0], ebuf.at[0], d2s.at[0], d2r, here).wait_send()
        remote(tokv, tokv, a1z, a1r.at[0], here).wait_send()

    @pl.when(k == 0)
    def _():
        remote(ebuf.at[0, 1], ebuf.at[0, 1], d2z, d2zr, here).wait_send()


def body(*args):
    rows, feat = args[0].shape
    hbm = pl.BlockSpec(memory_space=pl.ANY)
    smem = pl.BlockSpec(memory_space=pltpu.SMEM)
    blocks = args[9].shape[1]
    dma = pltpu.SemaphoreType.DMA
    return pl.pallas_call(
        kernel,
        out_shape=jax.ShapeDtypeStruct((rows, feat), BF16),
        in_specs=[hbm] * 7 + [smem] * 2 + [hbm],
        out_specs=pl.BlockSpec(memory_space=pltpu.VMEM),
        scratch_shapes=[
            pltpu.VMEM((ROWS, feat), BF16),
            pltpu.VMEM((STEPS, TOK, 2 * feat), BF16),
            pltpu.VMEM((2 * feat, COLD * BLOCK), BF16),
            pltpu.VMEM((2 * feat, COLD * BLOCK), BF16),
            pltpu.VMEM((2 * feat, 2 * BLOCK), BF16),
            pltpu.VMEM(((COLD + 1) * BLOCK, 2 * feat), BF16),
            pltpu.VMEM((STEPS * TOK, blocks), jnp.int32),
            pltpu.VMEM((STEPS, TOK, BLOCK), BF16),
            pltpu.VMEM((STEPS, SLOTS, TOK), BF16),
            pltpu.VMEM((STEPS, SLOTS, BLOCK), F32),
            pltpu.VMEM((STEPS, NZ, SLOTS, 2 * BLOCK), BF16),
            pltpu.VMEM((STEPS, NZ, SLOTS, 2 * BLOCK), F32),
            pltpu.VMEM((STEPS, NZ - 1, SLOTS, 2 * BLOCK), BF16),
            pltpu.VMEM((STEPS, NZ, SLOTS, BLOCK), BF16),
            pltpu.VMEM((STEPS, TOK, 2 * feat), BF16),
            pltpu.VMEM((STEPS, ROWS, 2 * feat), F32),
            pltpu.VMEM((STEPS, NX - 1, ROWS, 2 * feat), BF16),
            pltpu.VMEM((STEPS, 2, ROWS, feat), BF16),
            pltpu.VMEM((NY, ROWS, feat), BF16),
            dma, dma, dma((6,)), dma((6,)), dma((6,)),
            dma, dma, dma((STEPS,)), dma((STEPS,)), dma((STEPS,)),
            dma((STEPS,)), dma((STEPS,)), dma((STEPS,)), dma((STEPS,)),
            dma((STEPS,)), dma((STEPS,)), dma((STEPS,)), dma, dma, dma,
        ],
        compiler_params=pltpu.CompilerParams(collective_id=0, has_side_effects=True),
    )(*args)


def solution(mesh):
    return jax.shard_map(
        body,
        mesh=mesh,
        in_specs=(
            P("cold", "hot"),
            P("hot", "cold"),
            P("hot", "cold"),
            P("cold", "hot"),
            P("hot", "cold"),
            P("hot", "cold"),
            P("cold", "hot"),
            P(),
            P(),
            P(),
        ),
        out_specs=P("cold", "hot"),
        check_vma=False,
    )
```

time: 193 us -> 57.1 us (0.30); the launches traced: 190 us -> 56.8 us
  blocking collectives: 73.3 us -> 0 us
  waiting for transfers between devices: 65 us -> 0 us
  Pallas kernels: 0 us -> 53.5 us
  between operations: 15.7 us -> 0.01 us
  local copies, waits for them, and re-layouts: 14.9 us -> 3.33 us
  other arithmetic: 10.4 us -> 0 us
  starting transfers between devices: 6.39 us -> 0 us
  matrix products: 3.89 us -> 0 us
    reduce_scatter x1 -> x0, waiting for transfers between devices: 56 us -> none  [sum_packed(): lax.psum_scatter(lines, axis, tiled=True).reshape(-1)]
    all_to_all x2 -> x0, blocking collectives: 54.3 us -> none  [the longest x1 34.3 us: sum_at_owner(): lax.all_to_all(tiles, axis, split_axis=0, concat_axis=0, tiled=True)]
    pallas_call x0 -> x1, Pallas kernels: none -> 53.5 us  [body(): pl.pallas_call(kernel, out_shape=jax.ShapeDtypeStruct((rows, feat), BF16)...]
    all_gather x1 -> x0, blocking collectives: 19 us -> none  [gather_packed(): lines, at, finished = (lax.all_gather(line, axis), 0, [])]
    all_to_all x1 -> x0, waiting for transfers between devices: 9 us -> none  [sent_to_all(): return lax.all_to_all(copies, axis, split_axis=0, concat_axis=0, tiled=True)]
    all_to_all x1 -> x0, starting transfers between devices: 6.35 us -> none  [sent_to_all(): return lax.all_to_all(copies, axis, split_axis=0, concat_axis=0, tiled=True)]
    dot_general x6 -> x0, matrix products: 3.89 us -> none  [the longest x1 1.54 us: body(): cold_gates = jnp.dot(arrived, cold_gate, preferred_element_type=jnp.float32)]
    another operation x6 -> x0, local copies, waits for them, and re-layouts: 3.84 us -> none  [the longest x4 3.6 us: sum_packed(): lines = jnp.concatenate([b.reshape(size, -1) for b in tiles], axis=1)]
  transfers between devices with their start and end apart: 2 -> 0, of which waited for: 2 -> 0; matrix products, arithmetic and copies ran while one was open for 6% -> 0% of each run, Pallas kernels for 0% -> 0%
where the time goes in v1:
time: 57.1 us; the launch traced here: 56.8 us
  Pallas kernels  53.5 us (94%)
  local copies, waits for them, and re-layouts  3.33 us (6%)
    pallas_call x1, Pallas kernels, body(): pl.pallas_call(kernel, out_shape=jax.ShapeDtypeStruct((rows, feat), BF16)...  53.5 us
    unnamed x2, local copies, waits for them, and re-layouts  3.33 us

profile of v1, /device:TPU:1, one launch (start us, length us, event | category | flops | bytes accessed | tf_op | source)
XLA Modules:
  0.0 56.8 jit_solution(252017588452195500)
XLA Ops:
  0.0 2.0 %copy.11.mask = s32[512,224]{1,0:T(8,128)} copy(s32[512,224]{0,1:T(8,128)} %param.19) | data formatting | bytes 917504 | tf_op args[9]
  2.0 53.5 %shard_map.100 = bf16[16,512]{1,0:T(8,128)(2,1)} custom-call(bf16[16,512]{1,0:T(8,128)(2,1)} %tok.1, bf16[512,128]{1,0:T(8,128)(2,1)} %hot_gate.1, bf16[512,128]{1,0:T(8,128)(2,1)} %hot_up.1, bf16[128,512]{1,0:T(8,128)(2,1)} %hot_down.1, bf16[512,768]{1,0:T(8,128)(2,1)} %cold_gate.1, bf16[512,768]{1,0:T(8,128)(2,1)} %cold_up.1, bf16[768,512]{1,0:T(8,128)(2,1)} %cold_down.1, ...), custom_call_target="tpu_custom_call" | custom-call | tf_op jit(solution)/shard_map/pallas_call | solution.py:289
  55.5 1.3 %copy.13 = bf16[16,512]{1,0:T(8,128)(2,1)} copy(bf16[16,512]{1,0:T(8,128)(2,1)} %shard_map.100) | data formatting | bytes 32768

commit v2 on v1

v2 whole, which is shorter than its diff:
```python
import jax
import jax.numpy as jnp
from jax import lax
from jax.experimental import pallas as pl
from jax.experimental.pallas import tpu as pltpu
from jax.sharding import PartitionSpec as P

BLOCK = 128
NX, NY, NZ = 4, 8, 8
STEPS = 4
CAP = 8
ROWS = 16
TOK = NX * ROWS
SLOTS = NX * CAP
COLD = 6
F32, BF16 = jnp.float32, jnp.bfloat16
ORDER = ((0, 7, 5, 2), (1, 6, 4, 3))
CORE_OF = tuple(0 if dy in ORDER[0] else 1 for dy in range(NY))
SEND_ORDER = (0, 1, 7, 6, 2, 3, 5, 4)
OWN = ORDER[0].index(0)
FAR_FIRST = (4, 3, 5, 2, 6, 1, 7)
MESH = pl.DeviceIdType.MESH


def dot(a, b):
    return jnp.dot(a, b, preferred_element_type=F32)


def dot_t(a, b):
    return lax.dot_general(a, b, (((0,), (0,)), ((), ())), preferred_element_type=F32)


def kernel(
    tok, hot_gate, hot_up, hot_down, cold_gate, cold_up, cold_down, hot_ids, cold_ids, mask,
    out,
    tokv, xbuf, wcg, wcu, wh, wd, maskv, hot_s, cold_s, hits, units, ptab, pmat, mz, sbuf, sown, rbuf, hbuf, obuf, oown, dbuf, ebuf, fbuf,
    xy_in, z_in, tok_sem, mask_sem, ids_sem, wl_sem, ws_sem, wr_sem,
    a1s, a1z, a1r, a2s, a2r, bs, br, cs, cr, d1s, d1r, d2s, d2z, d2r, d2zr,
):
    hot, cold = lax.axis_index("hot"), lax.axis_index("cold")
    z, k = lax.div(hot, 2), lax.rem(hot, 2)
    x, y = lax.div(cold, NY), lax.rem(cold, NY)
    feat = tok.shape[1]

    def dev(px, py, pz, pk):
        return {"hot": pz * 2 + pk, "cold": px * NY + py}

    def at_x(d):
        return lax.rem(x + (d % NX), NX)

    def at_y(d):
        return lax.rem(y + NY + d, NY)

    def at_z(d):
        return lax.rem(z + (d % NZ), NZ)

    def dy_of(s):
        return ORDER[0][s] + k * (ORDER[1][s] - ORDER[0][s])

    def remote(src, dst, send, recv, to):
        return pltpu.make_async_remote_copy(
            src_ref=src, dst_ref=dst, send_sem=send, recv_sem=recv, device_id=to, device_id_type=MESH
        )

    here = dev(x, y, z, k)
    sister = dev(x, y, z, 1 - k)
    cols = pl.ds(pl.multiple_of(k * feat, feat), feat)
    mine = pl.ds(pl.multiple_of(k * feat, feat), feat)

    tok_load = pltpu.make_async_copy(tok, tokv, tok_sem)
    tok_load.start()

    barrier = pltpu.get_barrier_semaphore()

    def greet(to):
        pl.semaphore_signal(barrier, inc=1, device_id=to, device_id_type=MESH)

    greet(sister)
    for d in range(1, NY):
        greet(dev(x, at_y(d), z, 1))
    for d in range(1, NX):
        greet(dev(at_x(d), y, z, 1))
    for d in FAR_FIRST:
        greet(dev(x, y, at_z(d), 0))

    mask_load = pltpu.make_async_copy(mask, maskv, mask_sem)
    hot_load = pltpu.make_async_copy(hot_ids, hot_s, ids_sem.at[0])
    cold_load = pltpu.make_async_copy(cold_ids, cold_s, ids_sem.at[1])
    pieces = (
        (cold_gate, wcg.at[mine, :]),
        (cold_up, wcu.at[mine, :]),
        (hot_gate, wh.at[mine, pl.ds(0, BLOCK)]),
        (hot_up, wh.at[mine, pl.ds(BLOCK, BLOCK)]),
        (cold_down, wd.at[pl.ds(0, COLD * BLOCK), cols]),
        (hot_down, wd.at[pl.ds(COLD * BLOCK, BLOCK), cols]),
    )
    local_w = [pltpu.make_async_copy(a, b, wl_sem.at[i]) for i, (a, b) in enumerate(pieces)]
    remote_w = [remote(a, b, ws_sem.at[i], wr_sem.at[i], sister) for i, (a, b) in enumerate(pieces)]
    tok_load.wait()

    @pl.when(k == 1)
    def _():
        pl.semaphore_wait(barrier, 2 * (NY - 1) + 2 * (NX - 1) + 1)
        pl.semaphore_signal(xy_in, inc=1, device_id=sister, device_id_type=MESH)

    @pl.when(k == 0)
    def _():
        pl.semaphore_wait(xy_in, 1)

    for dy in SEND_ORDER:
        core = CORE_OF[dy]
        s = ORDER[core].index(dy)
        spot = xbuf.at[s, pl.ds(0, ROWS), cols]
        if dy:
            remote(tokv, spot, a1s, a1r.at[s], dev(x, at_y(-dy), z, core)).start()
        else:

            @pl.when(k == 0)
            def _():
                pltpu.make_async_copy(tok, xbuf.at[OWN, pl.ds(0, ROWS), pl.ds(0, feat)], a1r.at[OWN]).start()

            @pl.when(k == 1)
            def _():
                remote(
                    tokv, xbuf.at[OWN, pl.ds(0, ROWS), pl.ds(feat, feat)], a1z, a1r.at[OWN], sister
                ).start()

    for copy in (mask_load, hot_load, cold_load):
        copy.start()
    for copy in local_w[:4] + remote_w[:4] + local_w[4:]:
        copy.start()

    def spread(s):
        head = xbuf.at[s, pl.ds(0, ROWS), :]
        remote(head, head, a2s.at[s], a1r.at[s], here).wait_recv()
        for dx in (2, 1, 3):
            remote(
                head, xbuf.at[s, pl.ds(dx * ROWS, ROWS), :], a2s.at[s], a2r.at[s], dev(at_x(-dx), y, z, k)
            ).start()

    def gate_up(s):
        rest = xbuf.at[s, pl.ds(ROWS, TOK - ROWS), :]
        remote(rest, rest, a2s.at[s], a2r.at[s], here).wait_recv()
        if s == 0:
            for i in range(4):
                local_w[i].wait()
                remote_w[i].wait_recv()
        rows = xbuf[s]
        picked = dot(pmat[s], rows).astype(BF16)
        gates, ups = dot(picked, wcg[...]), dot(picked, wcu[...])
        hots = dot(rows, wh[...])
        for j in range(NZ):
            if j < COLD:
                part = slice(j * BLOCK, (j + 1) * BLOCK)
                gate, up = gates[:, part], ups[:, part]
            else:
                part = slice((j - COLD) * SLOTS, (j - COLD + 1) * SLOTS)
                gate, up = hots[part, :BLOCK], hots[part, BLOCK:]
            sown[s, j, :, :BLOCK] = gate
            sown[s, j, :, BLOCK:] = up
            sbuf[s, j, :, :BLOCK] = gate.astype(BF16)
            sbuf[s, j, :, BLOCK:] = up.astype(BF16)
        if s == 0:

            @pl.when(k == 0)
            def _():
                pl.semaphore_wait(barrier, 2 * (NZ - 1) + 1)
                pl.semaphore_signal(z_in, inc=1, device_id=sister, device_id_type=MESH)

            @pl.when(k == 1)
            def _():
                pl.semaphore_wait(z_in, 1)

        for dz in FAR_FIRST:
            remote(
                sbuf.at[s, at_z(dz)], rbuf.at[s, dz - 1], bs.at[s], br.at[s], dev(x, y, at_z(dz), k)
            ).start()

    def share(s):
        remote(rbuf.at[s], rbuf.at[s], bs.at[s], br.at[s], here).wait_recv()
        terms = sown[s, z]
        for i in range(NZ - 1):
            terms = terms + rbuf[s, i].astype(F32)
        gate, up = terms[:, :BLOCK], terms[:, BLOCK:]
        hidden = gate / (1.0 + jnp.exp(-gate)) * up * mz[s]
        hbuf[s, z] = hidden.astype(BF16)
        for dz in FAR_FIRST:
            remote(
                hbuf.at[s, z], hbuf.at[s, z], cs.at[s], cr.at[s], dev(x, y, at_z(dz), k)
            ).start()

    spread(0)

    for copy in (mask_load, hot_load, cold_load):
        copy.wait()
    bits = maskv[...].astype(F32).astype(BF16)
    blocks = maskv.shape[0]
    block_no = lax.broadcasted_iota(jnp.int32, (blocks, BLOCK), 0)
    cold_sel = jnp.zeros((blocks, BLOCK), F32)
    for j in range(COLD):
        cold_sel = cold_sel + jnp.where(block_no == cold_s[cold * COLD + j], 1.0, 0.0)
    unit_id = jnp.where(z < COLD, cold_s[cold * COLD + jnp.minimum(z, COLD - 1)], hot_s[cold])
    unit_sel = jnp.where(block_no == unit_id, 1.0, 0.0)
    hits[...] = jnp.minimum(dot_t(bits, cold_sel.astype(BF16)), 1.0)
    units[...] = dot_t(bits, unit_sel.astype(BF16))

    def in_order(ref):
        starts = [(at_x(dx) * NY + at_y(dy_of(s))) * ROWS for s in range(STEPS) for dx in range(NX)]
        return jnp.concatenate([ref[pl.ds(pl.multiple_of(i, ROWS), ROWS), :] for i in starts], axis=0)

    hit, unit_bit = in_order(hits), in_order(units)
    total = STEPS * TOK
    row = lax.broadcasted_iota(jnp.int32, (total, total), 0)
    col = lax.broadcasted_iota(jnp.int32, (total, total), 1)
    earlier = (lax.div(row, ROWS) == lax.div(col, ROWS)) & (col < row)
    slot = dot(jnp.where(earlier, 1.0, 0.0).astype(BF16), hit.astype(BF16))
    row = lax.broadcasted_iota(jnp.int32, (total, BLOCK), 0)
    lane = lax.broadcasted_iota(jnp.int32, (total, BLOCK), 1)
    base = lax.rem(lax.div(row, ROWS), NX) * CAP
    chosen = jnp.where((slot + base.astype(F32) == lane.astype(F32)) & (hit > 0.5), 1.0, 0.0)
    for s in range(STEPS):
        step_rows = slice(s * TOK, (s + 1) * TOK)
        pick = chosen[step_rows]
        ptab[s] = pick.astype(BF16)
        turned = jnp.transpose(pick)[:SLOTS].astype(BF16)
        pmat[s] = turned
        tokens_bit = unit_bit[step_rows]
        slot_bit = dot(turned, tokens_bit.astype(BF16))
        half_bit = jnp.where(z == COLD, tokens_bit[:SLOTS], tokens_bit[SLOTS:])
        mz[s] = jnp.where(z < COLD, slot_bit, half_bit)

    spread(1)
    gate_up(0)
    spread(3)
    spread(2)
    for copy in remote_w[4:]:
        copy.start()
    def down(s):
        most = hbuf.at[s, pl.ds(0, NZ - 1)]
        remote(most, most, cs.at[s], cr.at[s], here).wait_recv()
        if s == 0:
            for i in (4, 5):
                local_w[i].wait()
                remote_w[i].wait_recv()
        colds = jnp.concatenate([hbuf[s, j] for j in range(COLD)], axis=1)
        placed = dot(ptab[s][:, :SLOTS], colds).astype(BF16)
        hots = jnp.concatenate([hbuf[s, COLD], hbuf[s, COLD + 1]], axis=0)
        result = dot(placed, wd[: COLD * BLOCK, :]) + dot(hots, wd[COLD * BLOCK :, :])
        oown[s] = result[:ROWS]
        obuf[s] = result.astype(BF16)
        for dx in (2, 1, 3):
            remote(
                obuf.at[s, pl.ds(dx * ROWS, ROWS), :], dbuf.at[s, dx - 1], d1s.at[s], d1r.at[s],
                dev(at_x(dx), y, z, k),
            ).start()

    def collect(s):
        remote(dbuf.at[s], dbuf.at[s], d1s.at[s], d1r.at[s], here).wait_recv()
        terms = oown[s]
        for i in range(NX - 1):
            terms = terms + dbuf[s, i].astype(F32)
        ebuf[s, 0] = terms[:, :feat].astype(BF16)
        ebuf[s, 1] = terms[:, feat:].astype(BF16)
        dy = dy_of(s)

        def to_owners():
            for f in range(2):
                remote(
                    ebuf.at[s, f], fbuf.at[dy], d2s.at[s], d2r, dev(x, at_y(dy), z, f)
                ).start()

        if s != OWN:
            to_owners()
        else:
            pl.when(k == 1)(to_owners)

            @pl.when(k == 0)
            def _():
                remote(ebuf.at[OWN, 1], fbuf.at[0], d2z, d2zr, sister).start()
                fbuf[0] = terms[:, :feat].astype(BF16)

    gate_up(1)
    share(0)
    gate_up(2)
    share(1)
    gate_up(3)
    share(2)
    down(0)
    share(3)
    down(1)
    collect(0)
    down(2)
    down(3)
    collect(1)
    collect(2)
    collect(3)

    remote(fbuf.at[pl.ds(1, NY - 1)], fbuf.at[pl.ds(1, NY - 1)], a1s, d2r, here).wait_recv()

    @pl.when(k == 1)
    def _():
        remote(fbuf.at[0], fbuf.at[0], d2z, d2zr, here).wait_recv()

    answer = fbuf[0].astype(F32)
    for dy in range(1, NY):
        answer = answer + fbuf[dy].astype(F32)
    out[...] = answer.astype(BF16)

    seven = fbuf.at[pl.ds(1, NY - 1)]
    remote(seven, seven, a1s, d2r, here).wait_send()
    for copy in remote_w:
        copy.wait_send()
    for s in range(STEPS):
        rest = xbuf.at[s, pl.ds(ROWS, TOK - ROWS), :]
        remote(rest, rest, a2s.at[s], a2r.at[s], here).wait_send()
        remote(rbuf.at[s], rbuf.at[s], bs.at[s], br.at[s], here).wait_send()
        most = hbuf.at[s, pl.ds(0, NZ - 1)]
        remote(most, most, cs.at[s], cr.at[s], here).wait_send()
        remote(dbuf.at[s], dbuf.at[s], d1s.at[s], d1r.at[s], here).wait_send()
        if s != OWN:
            remote(ebuf.at[s], ebuf.at[s], d2s.at[s], d2r, here).wait_send()

    @pl.when(k == 1)
    def _():
        remote(ebuf.at[OWN], ebuf.at[OWN], d2s.at[OWN], d2r, here).wait_send()
        remote(tokv, tokv, a1z, a1r.at[OWN], here).wait_send()

    @pl.when(k == 0)
    def _():
        remote(ebuf.at[OWN, 1], ebuf.at[OWN, 1], d2z, d2zr, here).wait_send()


def body(*args):
    rows, feat = args[0].shape
    hbm = pl.BlockSpec(memory_space=pl.ANY)
    args = (*args[:9], args[9].T)
    blocks, tokens = args[9].shape
    dma = pltpu.SemaphoreType.DMA
    args = tuple(pltpu.with_memory_space_constraint(a, pltpu.HBM) for a in args)
    return pl.pallas_call(
        kernel,
        out_shape=jax.ShapeDtypeStruct((rows, feat), BF16),
        in_specs=[hbm] * 10,
        out_specs=pl.BlockSpec(memory_space=pltpu.VMEM),
        scratch_shapes=[
            pltpu.VMEM((ROWS, feat), BF16),
            pltpu.VMEM((STEPS, TOK, 2 * feat), BF16),
            pltpu.VMEM((2 * feat, COLD * BLOCK), BF16),
            pltpu.VMEM((2 * feat, COLD * BLOCK), BF16),
            pltpu.VMEM((2 * feat, 2 * BLOCK), BF16),
            pltpu.VMEM(((COLD + 1) * BLOCK, 2 * feat), BF16),
            pltpu.VMEM((blocks, tokens), jnp.int32),
            pltpu.SMEM(args[7].shape, jnp.int32),
            pltpu.SMEM(args[8].shape, jnp.int32),
            pltpu.VMEM((tokens, BLOCK), F32),
            pltpu.VMEM((tokens, BLOCK), F32),
            pltpu.VMEM((STEPS, TOK, BLOCK), BF16),
            pltpu.VMEM((STEPS, SLOTS, TOK), BF16),
            pltpu.VMEM((STEPS, SLOTS, BLOCK), F32),
            pltpu.VMEM((STEPS, NZ, SLOTS, 2 * BLOCK), BF16),
            pltpu.VMEM((STEPS, NZ, SLOTS, 2 * BLOCK), F32),
            pltpu.VMEM((STEPS, NZ - 1, SLOTS, 2 * BLOCK), BF16),
            pltpu.VMEM((STEPS, NZ, SLOTS, BLOCK), BF16),
            pltpu.VMEM((STEPS, TOK, 2 * feat), BF16),
            pltpu.VMEM((STEPS, ROWS, 2 * feat), F32),
            pltpu.VMEM((STEPS, NX - 1, ROWS, 2 * feat), BF16),
            pltpu.VMEM((STEPS, 2, ROWS, feat), BF16),
            pltpu.VMEM((NY, ROWS, feat), BF16),
            pltpu.SemaphoreType.REGULAR, pltpu.SemaphoreType.REGULAR,
            dma, dma, dma((2,)), dma((6,)), dma((6,)), dma((6,)),
            dma, dma, dma((STEPS,)), dma((STEPS,)), dma((STEPS,)),
            dma((STEPS,)), dma((STEPS,)), dma((STEPS,)), dma((STEPS,)),
            dma((STEPS,)), dma((STEPS,)), dma((STEPS,)), dma, dma, dma,
        ],
        compiler_params=pltpu.CompilerParams(collective_id=0, has_side_effects=True, vmem_limit_bytes=32 * 2**20),
    )(*args)


def solution(mesh):
    return jax.shard_map(
        body,
        mesh=mesh,
        in_specs=(
            P("cold", "hot"),
            P("hot", "cold"),
            P("hot", "cold"),
            P("cold", "hot"),
            P("hot", "cold"),
            P("hot", "cold"),
            P("cold", "hot"),
            P(),
            P(),
            P(),
        ),
        out_specs=P("cold", "hot"),
        check_vma=False,
    )
```

time: 57.1 us -> 51.4 us (0.900)
  Pallas kernels: 53.5 us -> 50.5 us
  local copies, waits for them, and re-layouts: 3.33 us -> 0.61 us
    pallas_call x1, Pallas kernels: 53.5 us -> 50.5 us  [body(): pl.pallas_call(kernel, out_shape=jax.ShapeDtypeStruct((rows, feat), BF16)...]
    unnamed x2 -> x1, local copies, waits for them, and re-layouts: 3.33 us -> 0.61 us
where the time goes in v2:
time: 51.4 us; the launch traced here: 51.1 us
  Pallas kernels  50.5 us (98%)
  local copies, waits for them, and re-layouts  0.61 us (1%)
    pallas_call x1, Pallas kernels, body(): pl.pallas_call(kernel, out_shape=jax.ShapeDtypeStruct((rows, feat), BF16)...  50.5 us

profile of v2, /device:TPU:1, one launch (start us, length us, event | category | flops | bytes accessed | tf_op | source)
XLA Modules:
  0.0 51.1 jit_solution(7988914098546763861)
XLA Ops:
  0.0 50.5 %shard_map.100 = bf16[16,512]{1,0:T(8,128)(2,1)S(1)} custom-call(bf16[16,512]{1,0:T(8,128)(2,1)} %tok.1, bf16[512,128]{1,0:T(8,128)(2,1)} %hot_gate.1, bf16[512,128]{1,0:T(8,128)(2,1)} %hot_up.1, bf16[128,512]{1,0:T(8,128)(2,1)} %hot_down.1, bf16[512,768]{1,0:T(8,128)(2,1)} %cold_gate.1, bf16[512,768]{1,0:T(8,128)(2,1)} %cold_up.1, ...), custom_call_target="tpu_custom_call" | custom-call | tf_op jit(solution)/shard_map/pallas_call | solution.py:340
  50.5 0.6 %copy.12 = bf16[16,512]{1,0:T(8,128)(2,1)} copy(bf16[16,512]{1,0:T(8,128)(2,1)S(1)} %shard_map.100) | data formatting | bytes 32768

commit v3 on v2

--- a/solution.py
+++ b/solution.py
@@ -18,6 +18,7 @@
 CORE_OF = tuple(0 if dy in ORDER[0] else 1 for dy in range(NY))
 SEND_ORDER = (0, 1, 7, 6, 2, 3, 5, 4)
 OWN = ORDER[0].index(0)
+LAST = STEPS - 1
 FAR_FIRST = (4, 3, 5, 2, 6, 1, 7)
 MESH = pl.DeviceIdType.MESH
 
@@ -61,6 +62,11 @@
         return pltpu.make_async_remote_copy(
             src_ref=src, dst_ref=dst, send_sem=send, recv_sem=recv, device_id=to, device_id_type=MESH
         )
+
+    def parts_of(s):
+        if s == LAST:
+            return ((STEPS, slice(feat, 2 * feat)), (s, slice(0, feat)))
+        return ((s, slice(0, 2 * feat)),)
 
     here = dev(x, y, z, k)
     sister = dev(x, y, z, 1 - k)
@@ -184,10 +190,9 @@
         gate, up = terms[:, :BLOCK], terms[:, BLOCK:]
         hidden = gate / (1.0 + jnp.exp(-gate)) * up * mz[s]
         hbuf[s, z] = hidden.astype(BF16)
-        for dz in FAR_FIRST:
-            remote(
-                hbuf.at[s, z], hbuf.at[s, z], cs.at[s], cr.at[s], dev(x, y, at_z(dz), k)
-            ).start()
+        for i in range(NZ - 1):
+            to = i + jnp.where(z <= i, 1, 0)
+            remote(hbuf.at[s, z], hbuf.at[s, z], cs.at[s], cr.at[s], dev(x, y, to, k)).start()
 
     spread(0)
 
@@ -245,23 +250,35 @@
         colds = jnp.concatenate([hbuf[s, j] for j in range(COLD)], axis=1)
         placed = dot(ptab[s][:, :SLOTS], colds).astype(BF16)
         hots = jnp.concatenate([hbuf[s, COLD], hbuf[s, COLD + 1]], axis=0)
-        result = dot(placed, wd[: COLD * BLOCK, :]) + dot(hots, wd[COLD * BLOCK :, :])
-        oown[s] = result[:ROWS]
-        obuf[s] = result.astype(BF16)
-        for dx in (2, 1, 3):
-            remote(
-                obuf.at[s, pl.ds(dx * ROWS, ROWS), :], dbuf.at[s, dx - 1], d1s.at[s], d1r.at[s],
-                dev(at_x(dx), y, z, k),
-            ).start()
+        for index, part in parts_of(s):
+            result = dot(placed, wd[: COLD * BLOCK, part]) + dot(hots, wd[COLD * BLOCK :, part])
+            oown[s, :, part] = result[:ROWS]
+            obuf[s, :, part] = result.astype(BF16)
+            for dx in (2, 1, 3):
+                remote(
+                    obuf.at[s, pl.ds(dx * ROWS, ROWS), part], dbuf.at[s, dx - 1, :, part], d1s.at[index],
+                    d1r.at[index], dev(at_x(dx), y, z, k),
+                ).start()
 
     def collect(s):
-        remote(dbuf.at[s], dbuf.at[s], d1s.at[s], d1r.at[s], here).wait_recv()
-        terms = oown[s]
-        for i in range(NX - 1):
-            terms = terms + dbuf[s, i].astype(F32)
-        ebuf[s, 0] = terms[:, :feat].astype(BF16)
-        ebuf[s, 1] = terms[:, feat:].astype(BF16)
         dy = dy_of(s)
+        for index, part in parts_of(s):
+            sums = dbuf.at[s, :, :, part]
+            remote(sums, sums, d1s.at[index], d1r.at[index], here).wait_recv()
+            terms = oown[s, :, part]
+            for i in range(NX - 1):
+                terms = terms + dbuf[s, i, :, part].astype(F32)
+            for f in range(2):
+                if index == s and s == LAST and f == 1:
+                    continue
+                if index != s and f == 0:
+                    continue
+                piece = terms[:, f * feat : (f + 1) * feat] if terms.shape[1] > feat else terms
+                ebuf[s, f] = piece.astype(BF16)
+                if s == LAST:
+                    remote(ebuf.at[s, f], fbuf.at[dy], d2s.at[s], d2r, dev(x, at_y(dy), z, f)).start()
+        if s == LAST:
+            return
 
         def to_owners():
             for f in range(2):
@@ -277,7 +294,7 @@
             @pl.when(k == 0)
             def _():
                 remote(ebuf.at[OWN, 1], fbuf.at[0], d2z, d2zr, sister).start()
-                fbuf[0] = terms[:, :feat].astype(BF16)
+                fbuf[0] = ebuf[OWN, 0]
 
     gate_up(1)
     share(0)
@@ -316,7 +333,9 @@
         remote(rbuf.at[s], rbuf.at[s], bs.at[s], br.at[s], here).wait_send()
         most = hbuf.at[s, pl.ds(0, NZ - 1)]
         remote(most, most, cs.at[s], cr.at[s], here).wait_send()
-        remote(dbuf.at[s], dbuf.at[s], d1s.at[s], d1r.at[s], here).wait_send()
+        for index, part in parts_of(s):
+            sums = dbuf.at[s, :, :, part]
+            remote(sums, sums, d1s.at[index], d1r.at[index], here).wait_send()
         if s != OWN:
             remote(ebuf.at[s], ebuf.at[s], d2s.at[s], d2r, here).wait_send()
 
@@ -370,7 +389,7 @@
             dma, dma, dma((2,)), dma((6,)), dma((6,)), dma((6,)),
             dma, dma, dma((STEPS,)), dma((STEPS,)), dma((STEPS,)),
             dma((STEPS,)), dma((STEPS,)), dma((STEPS,)), dma((STEPS,)),
-            dma((STEPS,)), dma((STEPS,)), dma((STEPS,)), dma, dma, dma,
+            dma((STEPS + 1,)), dma((STEPS + 1,)), dma((STEPS,)), dma, dma, dma,
         ],
         compiler_params=pltpu.CompilerParams(collective_id=0, has_side_effects=True, vmem_limit_bytes=32 * 2**20),
     )(*args)

time: 51.4 us -> 50.7 us (0.986)
  Pallas kernels: 50.5 us -> 49.8 us
    pallas_call x1, Pallas kernels: 50.5 us -> 49.8 us  [body(): pl.pallas_call(kernel, out_shape=jax.ShapeDtypeStruct((rows, feat), BF16)...]
where the time goes in v3:
time: 50.7 us; the launch traced here: 50.4 us
  Pallas kernels  49.8 us (98%)
  local copies, waits for them, and re-layouts  0.61 us (1%)
    pallas_call x1, Pallas kernels, body(): pl.pallas_call(kernel, out_shape=jax.ShapeDtypeStruct((rows, feat), BF16)...  49.8 us

profile of v3, /device:TPU:1, one launch (start us, length us, event | category | flops | bytes accessed | tf_op | source)
XLA Modules:
  0.0 50.4 jit_solution(10020197456812741285)
XLA Ops:
  0.0 49.8 %shard_map.100 = bf16[16,512]{1,0:T(8,128)(2,1)S(1)} custom-call(bf16[16,512]{1,0:T(8,128)(2,1)} %tok.1, bf16[512,128]{1,0:T(8,128)(2,1)} %hot_gate.1, bf16[512,128]{1,0:T(8,128)(2,1)} %hot_up.1, bf16[128,512]{1,0:T(8,128)(2,1)} %hot_down.1, bf16[512,768]{1,0:T(8,128)(2,1)} %cold_gate.1, bf16[512,768]{1,0:T(8,128)(2,1)} %cold_up.1, ...), custom_call_target="tpu_custom_call" | custom-call | tf_op jit(solution)/shard_map/pallas_call | solution.py:359
  49.8 0.6 %copy.12 = bf16[16,512]{1,0:T(8,128)(2,1)} copy(bf16[16,512]{1,0:T(8,128)(2,1)S(1)} %shard_map.100) | data formatting | bytes 32768

commit v4 on v3

--- a/solution.py
+++ b/solution.py
@@ -14,7 +14,7 @@
 SLOTS = NX * CAP
 COLD = 6
 F32, BF16 = jnp.float32, jnp.bfloat16
-ORDER = ((0, 7, 5, 2), (1, 6, 4, 3))
+ORDER = ((0, 7, 5, 2), (1, 3, 4, 6))
 CORE_OF = tuple(0 if dy in ORDER[0] else 1 for dy in range(NY))
 SEND_ORDER = (0, 1, 7, 6, 2, 3, 5, 4)
 OWN = ORDER[0].index(0)

time: 50.7 us -> 50.3 us (level)
  no operation moved by 1% of the time
where the time goes in v4:
time: 50.3 us; the launch traced here: 50.1 us
  Pallas kernels  49.4 us (98%)
  local copies, waits for them, and re-layouts  0.61 us (1%)
    pallas_call x1, Pallas kernels, body(): pl.pallas_call(kernel, out_shape=jax.ShapeDtypeStruct((rows, feat), BF16)...  49.4 us

profile of v4, /device:TPU:1, one launch (start us, length us, event | category | flops | bytes accessed | tf_op | source)
XLA Modules:
  0.0 50.1 jit_solution(3654585261721542214)
XLA Ops:
  0.0 49.4 %shard_map.100 = bf16[16,512]{1,0:T(8,128)(2,1)S(1)} custom-call(bf16[16,512]{1,0:T(8,128)(2,1)} %tok.1, bf16[512,128]{1,0:T(8,128)(2,1)} %hot_gate.1, bf16[512,128]{1,0:T(8,128)(2,1)} %hot_up.1, bf16[128,512]{1,0:T(8,128)(2,1)} %hot_down.1, bf16[512,768]{1,0:T(8,128)(2,1)} %cold_gate.1, bf16[512,768]{1,0:T(8,128)(2,1)} %cold_up.1, ...), custom_call_target="tpu_custom_call" | custom-call | tf_op jit(solution)/shard_map/pallas_call | solution.py:359
  49.5 0.6 %copy.12 = bf16[16,512]{1,0:T(8,128)(2,1)} copy(bf16[16,512]{1,0:T(8,128)(2,1)S(1)} %shard_map.100) | data formatting | bytes 32768
